TPU v7x, 32 devices: a whole 2x2x4 slice. The times are simulated.
32 devices in a mesh: seq: 8 (over z, x), fsdp: 4 (over y, core).
Axes of the slice: x: 2, y: 2, z: 4, core: 2. Of those that a mesh axis runs over, the one named last changes fastest.
Arguments:
- tokens: bfloat16 [4, 1024, 1536], P('fsdp', 'seq'), may hold values from -6 to 6
- in_weight: bfloat16 [1536, 6400], P('fsdp'), may hold values from -0.15625 to 0.15625
- step_weight: bfloat16 [1536, 48], P('fsdp'), may hold values from -0.15625 to 0.15625
- conv_kernel: bfloat16 [4, 3328], P(None, 'fsdp'), may hold values from -3 to 3
- conv_bias: bfloat16 [3328], P('fsdp'), may hold values from -3 to 3
- step_bias: bfloat16 [48], P('fsdp'), may hold values from -6 to -3
- log_decay: bfloat16 [48], P('fsdp'), may hold values from -7 to 1
- skip_gain: bfloat16 [48], P('fsdp'), may hold values from 0.5 to 1.5
- gate_gain: bfloat16 [3072], P('fsdp'), may hold values from 0.5 to 1.5
- norm_gain: bfloat16 [1536], P('fsdp'), may hold values from 0.5 to 1.5
- out_weight: bfloat16 [3072, 1536], P('fsdp'), may hold values from -0.109375 to 0.109375
- cotangent: bfloat16 [4, 1024, 1536], P('fsdp', 'seq'), may hold values from -6 to 6
Outputs:
- block_out: bfloat16 [4, 1024, 1536], P('fsdp', 'seq')
- input_grad: float32 [4, 1024, 1536], P('fsdp', 'seq')
- in_weight_grad: float32 [1536, 6400], P('fsdp')
- step_weight_grad: float32 [1536, 48], P('fsdp')
- conv_kernel_grad: float32 [4, 3328], P(None, 'fsdp')
- conv_bias_grad: float32 [3328], P('fsdp')
- step_bias_grad: float32 [48], P('fsdp')
- log_decay_grad: float32 [48], P('fsdp')
- skip_gain_grad: float32 [48], P('fsdp')
- gate_gain_grad: float32 [3072], P('fsdp')
- norm_gain_grad: float32 [1536], P('fsdp')
- out_weight_grad: float32 [3072, 1536], P('fsdp')
All inputs are finite; a program needn't handle non-finite values.
Results may differ from a plain program's by a relative error of at most 0.012.
The roundings to bfloat16 on the way count: a program that leaves them out, or rounds other values in their place, can miss the bound.
Values may be sent and summed in bfloat16 or wider, within the bound.
A program may use at most 320 MiB of HBM per device.

v0:
```python
import jax
import jax.numpy as jnp
from jax import lax
from jax.sharding import PartitionSpec as P

N = 128
BLOCK = 256
epsilon = 1e-05
bf16 = jnp.bfloat16
f32 = jnp.float32


def block_step(carried, pieces, decay_rate):
    x_blk, step_blk, b_blk, c_blk = pieces
    cumulative = jnp.cumsum(step_blk * decay_rate[None, :], axis=0).T
    positions = jnp.arange(step_blk.shape[0])
    triangle = positions[:, None] >= positions[None, :]
    log_gap = jnp.where(triangle[None], cumulative[:, :, None] - cumulative[:, None, :], -1e30)
    scores = jnp.dot(c_blk, b_blk.T)
    mixing = jnp.exp(log_gap) * scores[None] * step_blk.T[:, None, :]
    y_inside = jnp.einsum("hij,jhp->ihp", mixing, x_blk)
    y_carried = jnp.exp(cumulative).T[:, :, None] * jnp.einsum("in,hpn->ihp", c_blk, carried)
    weighting = jnp.exp(cumulative[:, -1:] - cumulative) * step_blk.T
    renewed = jnp.exp(cumulative[:, -1])[:, None, None] * carried + jnp.einsum(
        "hj,jhp,jn->hpn", weighting, x_blk, b_blk
    )
    return (renewed, y_inside + y_carried)


def ssd_scan(x_heads, step_size, decay_rate, b_conv, c_conv, carried):
    length = step_size.shape[0]
    extent = min(BLOCK, length)
    number = length // extent
    pieces = (
        x_heads.reshape((number, extent) + x_heads.shape[1:]),
        step_size.reshape((number, extent) + step_size.shape[1:]),
        b_conv.reshape(number, extent, -1),
        c_conv.reshape(number, extent, -1),
    )
    outs = []
    for k in range(number):
        carried, out = block_step(carried, tuple((p[k] for p in pieces)), decay_rate)
        outs.append(out)
    return jnp.concatenate(outs, 0).reshape(x_heads.shape)


def prepare(extended, raw_steps, conv_kernel, conv_offset, step_bias, log_rates):
    kernel_width = conv_kernel.shape[0]
    length = extended.shape[0] - kernel_width + 1
    summed = conv_offset[None, :] + sum(
        (
            conv_kernel[offset][None, :] * extended[offset : offset + length]
            for offset in range(kernel_width)
        )
    )
    active = jax.nn.silu(summed)
    split_at = active.shape[1] - 2 * N
    step_size = jax.nn.softplus(raw_steps + step_bias[None, :])
    return (
        active[:, :split_at],
        active[:, split_at : split_at + N],
        active[:, split_at + N :],
        step_size,
        -jnp.exp(log_rates),
    )


def mix_out(x_conv, b_conv, c_conv, step_size, decay_rate, gate_in, skip_part, carried):
    length, head_count = step_size.shape
    x_heads = x_conv.reshape(length, head_count, -1)
    result = (
        ssd_scan(x_heads, step_size, decay_rate, b_conv, c_conv, carried)
        + skip_part[None, :, None] * x_heads
    )
    return result.reshape(length, -1) * jax.nn.silu(gate_in)


def contract(left, right, left_dim, right_dim):
    return lax.dot_general(
        left, right, (((left_dim,), (right_dim,)), ((), ())), preferred_element_type=f32
    )


def shards(
    tokens,
    in_weight,
    step_weight,
    conv_kernel,
    conv_bias,
    step_bias,
    log_decay,
    skip_gain,
    gate_gain,
    norm_gain,
    out_weight,
    cotangent,
):
    seqs = lax.axis_size("seq")
    fs = lax.axis_size("fsdp")
    pos = lax.axis_index("seq")
    fpos = lax.axis_index("fsdp")
    heads = step_weight.shape[1]
    inner = out_weight.shape[0] * fs
    width = tokens.shape[-1]
    hg = heads // seqs
    cols = inner // seqs
    col = pos * cols
    KW, conv_l = conv_kernel.shape

    def sl(a, start, size, axis):
        return lax.dynamic_slice_in_dim(a, start, size, axis)

    w_part = jnp.concatenate(
        [
            sl(in_weight, col, cols, 1),
            sl(in_weight, inner + col, cols, 1),
            in_weight[:, 2 * inner :],
            sl(step_weight, pos * hg, hg, 1),
        ],
        axis=1,
    )
    w_g = lax.all_gather(w_part, "fsdp", axis=0, tiled=True)
    small = jnp.concatenate(
        [conv_kernel.reshape(-1), conv_bias, step_bias, log_decay, skip_gain, gate_gain, norm_gain]
    )
    small = lax.all_gather(small, "fsdp", axis=0, tiled=False).astype(f32)
    at = [0]

    def take(n):
        r = small[:, at[0] : at[0] + n]
        at[0] += n
        return r

    kernel_f = take(KW * conv_l).reshape(fs, KW, conv_l).transpose(1, 0, 2).reshape(KW, -1)
    bias_f = take(conv_l).reshape(-1)
    step_bias_f = take(heads // fs).reshape(-1)
    decay_f = take(heads // fs).reshape(-1)
    skip_f = take(heads // fs).reshape(-1)
    gate_f = sl(take(inner // fs).reshape(-1), col, cols, 0)
    norm_f = take(width // fs).reshape(-1)
    tok = lax.all_gather(tokens[0], "seq", axis=0, tiled=True)
    cot = lax.all_gather(cotangent[0], "seq", axis=0, tiled=True)
    w_out = lax.all_gather(out_weight, "fsdp", axis=0, tiled=True)
    w_out_g = sl(w_out, col, cols, 0)
    length = tok.shape[0]
    own = length // seqs
    resid = tok.astype(f32)
    scale_in = lax.rsqrt(jnp.mean(resid * resid, axis=-1, keepdims=True) + epsilon)
    hidden = (resid * scale_in * norm_f[None]).astype(bf16)
    proj = contract(hidden, w_g, 1, 0).astype(bf16).astype(f32)
    gate_in = proj[:, :cols]
    body = proj[:, cols : 2 * cols + 2 * N]
    raw = proj[:, 2 * cols + 2 * N :]
    my_kernel = jnp.concatenate([sl(kernel_f, col, cols, 1), kernel_f[:, inner:]], axis=1)
    my_bias = jnp.concatenate([sl(bias_f, col, cols, 0), bias_f[inner:]], axis=0)
    my_step_bias = sl(step_bias_f, pos * hg, hg, 0)
    my_decay = sl(decay_f, pos * hg, hg, 0)
    my_skip = sl(skip_f, pos * hg, hg, 0)
    extended = jnp.concatenate([jnp.zeros((KW - 1, cols + 2 * N), f32), body], axis=0)
    prepared, pull_prepare = jax.vjp(
        prepare, extended, raw, my_kernel, my_bias, my_step_bias, my_decay
    )
    x_conv, b_conv, c_conv, step_size, decay_rate = prepared
    start = jnp.zeros((hg, cols // hg, N), f32)
    gated_f, pull_mix = jax.vjp(
        mix_out, x_conv, b_conv, c_conv, step_size, decay_rate, gate_in, my_skip, start
    )
    gated_b = gated_f.astype(bf16)
    gated = gated_b.astype(f32)
    mixed_grad = contract(cot, w_out_g, 1, 1)
    g = mixed_grad * gate_f[None]
    stats = jnp.stack([jnp.sum(gated * gated, axis=1), jnp.sum(g * gated, axis=1)])
    stats = lax.psum(stats, "seq") / inner
    scale_out = lax.rsqrt(stats[0] + epsilon)[:, None]
    mixed_norm = (gated * scale_out * gate_f[None]).astype(bf16)
    gate_gain_grad = jnp.sum(mixed_grad * gated * scale_out, axis=0)
    gated_grad = (scale_out * g - scale_out**3 * gated * stats[1][:, None]).astype(bf16)
    mixed_all = lax.all_to_all(mixed_norm, "seq", split_axis=0, concat_axis=1, tiled=True)
    my_tok = tokens[0].astype(f32)
    block_out = (my_tok + contract(mixed_all, w_out, 1, 0)).astype(bf16)
    out_part = contract(mixed_norm, cot, 0, 0)
    x_grad, b_grad, c_grad, step_grad, rate_grad, gate_grad, skip_grad, _ = pull_mix(
        gated_grad.astype(f32)
    )
    ext_grad, raw_grad, kernel_grad, bias_grad, step_bias_grad, decay_grad = pull_prepare(
        (x_grad, b_grad, c_grad, step_grad, rate_grad)
    )
    proj_grad = jnp.concatenate([gate_grad, ext_grad[KW - 1 :], raw_grad], axis=1).astype(bf16)
    hid_part = contract(proj_grad, w_g, 1, 1)
    hidden_grad = lax.psum_scatter(
        hid_part.astype(bf16), "seq", scatter_dimension=0, tiled=True
    ).astype(f32)
    in_part = contract(hidden, proj_grad, 0, 0)
    in_red = lax.psum_scatter(in_part.astype(bf16), "fsdp", scatter_dimension=0, tiled=True)
    in_all = lax.all_gather(in_red, "seq", axis=0, tiled=False).astype(f32)
    in_grad = jnp.concatenate(
        [
            jnp.moveaxis(in_all[:, :, :cols], 0, 1).reshape(-1, inner),
            jnp.moveaxis(in_all[:, :, cols : 2 * cols], 0, 1).reshape(-1, inner),
            jnp.sum(in_all[:, :, 2 * cols : 2 * cols + 2 * N], axis=0),
        ],
        axis=1,
    )
    step_w_grad = jnp.moveaxis(in_all[:, :, 2 * cols + 2 * N :], 0, 1).reshape(-1, heads)
    out_red = lax.psum_scatter(out_part.astype(bf16), "fsdp", scatter_dimension=0, tiled=True)
    out_all = lax.all_gather(out_red, ("seq", "fsdp"), axis=0, tiled=True)
    out_rows = inner // fs
    out_grad = sl(out_all, fpos * out_rows, out_rows, 0).astype(f32)
    own_scale = lax.rsqrt(jnp.mean(my_tok * my_tok, axis=-1, keepdims=True) + epsilon)
    norm_gain_grad = jnp.sum(hidden_grad * my_tok * own_scale, axis=0)
    e = hidden_grad * norm_f[None]
    inner_mean = jnp.mean(e * my_tok, axis=-1, keepdims=True)
    input_grad = cotangent[0].astype(f32) + own_scale * e - own_scale**3 * my_tok * inner_mean

    def put(a, total, start, axis):
        shape = list(a.shape)
        shape[axis] = total
        idx = [0] * a.ndim
        idx[axis] = start
        return lax.dynamic_update_slice(jnp.zeros(shape, f32), a, tuple(idx))

    conv = inner + 2 * N
    kg = jnp.concatenate([put(kernel_grad[:, :cols], inner, col, 1), kernel_grad[:, cols:]], 1)
    bg = jnp.concatenate([put(bias_grad[:cols], inner, col, 0), bias_grad[cols:]], 0)
    packed = jnp.concatenate(
        [
            kg.reshape(-1),
            bg,
            put(step_bias_grad, heads, pos * hg, 0),
            put(decay_grad, heads, pos * hg, 0),
            put(skip_grad, heads, pos * hg, 0),
            put(gate_gain_grad, inner, col, 0),
            norm_gain_grad,
        ]
    )
    packed = lax.psum(packed, ("seq", "fsdp"))
    at[0] = 0

    def grab(n, size, rows=None):
        r = packed[at[0] : at[0] + n]
        at[0] += n
        if rows:
            return sl(r.reshape(rows, -1), fpos * size, size, 1)
        return sl(r, fpos * size, size, 0)

    kernel_out = grab(KW * conv, conv_l, KW)
    bias_out = grab(conv, conv_l)
    sb_out = grab(heads, heads // fs)
    ld_out = grab(heads, heads // fs)
    sk_out = grab(heads, heads // fs)
    gg_out = grab(inner, inner // fs)
    ng_out = grab(width, width // fs)
    return (
        block_out[None],
        input_grad[None],
        in_grad,
        step_w_grad,
        kernel_out,
        bias_out,
        sb_out,
        ld_out,
        sk_out,
        gg_out,
        ng_out,
        out_grad,
    )


def solution(mesh):
    row = P("fsdp", None)
    tok = P("fsdp", "seq", None)
    one = P("fsdp")
    return jax.shard_map(
        shards,
        mesh=mesh,
        in_specs=(tok, row, row, P(None, "fsdp"), one, one, one, one, one, one, row, tok),
        out_specs=(tok, tok, row, row, P(None, "fsdp"), one, one, one, one, one, one, row),
        check_vma=False,
    )
```

profile of v0, /device:TPU:0, one launch (start us, length us, event | category | flops | bytes accessed | tf_op | source)
XLA Modules:
  0.0 861.9 jit_solution(4475649698283908109)
XLA Ops:
  13.7 13.6 %all-reduce.34 = bf16[21392]{0:T(1024)(128)(2,1)S(1)} all-reduce(bf16[21392]{0:T(1024)(128)(2,1)S(1)} %dynamic-update-slice), channel_id=2, replica_groups=mesh['seq'=8,'fsdp'=4] {'fsdp'}, use_global_device_ids=true, to_apply=%add.34 | all-reduce | flops 21392 | bytes 85568
  30.7 42.3 %all-gather.17.cloned.1.call-done = bf16[1,1024,1536]{2,1,0:T(8,128)(2,1)} async-done(((bf16[1,128,1536]{2,1,0:T(8,128)(2,1)}), bf16[1,1024,1536]{2,1,0:T(8,128)(2,1)}) %all-gather.17.cloned.1.call-update) | async-done | bytes 3145744 | tf_op jit(solution)/shard_map/all_gather | solution.py:141
  75.8 28.8 %all-gather.11.cloned.1.call-done = bf16[1536,1030]{1,0:T(8,128)(2,1)} async-done(((bf16[384,1030]{1,0:T(8,128)(2,1)}), bf16[1536,1030]{1,0:T(8,128)(2,1)}) %all-gather.11.cloned.1.call-update) | async-done | bytes 3164176 | tf_op jit(solution)/shard_map/all_gather | solution.py:122
  134.5 32.4 %all-gather.19.cloned.1.call-done = bf16[1,1024,1536]{2,1,0:T(8,128)(2,1)} async-done(((bf16[1,128,1536]{2,1,0:T(8,128)(2,1)}), bf16[1,1024,1536]{2,1,0:T(8,128)(2,1)}) %all-gather.19.cloned.1.call-update) | async-done | bytes 3145744 | tf_op jit(solution)/shard_map/all_gather | solution.py:142
  166.9 64.3 %all-gather.13.cloned.1.call-done = bf16[3072,1536]{1,0:T(8,128)(2,1)} async-done(((bf16[768,1536]{1,0:T(8,128)(2,1)}), bf16[3072,1536]{1,0:T(8,128)(2,1)}) %all-gather.13.cloned.1.call-update) | async-done | bytes 9437200 | tf_op jit(solution)/shard_map/all_gather | solution.py:143
  237.9 22.3 %psum.14 = f32[2,1024]{1,0:T(2,128)} all-reduce(f32[2,1024]{1,0:T(2,128)} %pad_maximum_fusion.6), channel_id=1, replica_groups=mesh['seq'=8,'fsdp'=4] {'seq'}, use_global_device_ids=true, to_apply=%region_11.12 | all-reduce | flops 2048 | bytes 16384 | tf_op jit(solution)/shard_map/psum | solution.py:173
  294.6 6.8 fusion.118
  302.8 7.5 reduce-window.70
  313.3 8.2 reduce-window.76
  330.9 7.6 reduce-window.74
  340.1 15.3 %reduce-window.66 = f32[6,2,128]{2,1,0:T(2,128)S(1)} reduce-window(f32[6,2,128]{2,1,0:T(2,128)S(1)} %reshape.527, f32[]{:T(128)} %constant.35.clone.1), window={size=1x1x128 pad=0_0x0_0x0_127}, to_apply=%region_21.22 | reduce-window | flops 195072 | bytes 12292 | tf_op jit(solution)/shard_map/reduce-window.8
  373.8 8.0 multiply_reduce_fusion.2
  392.5 6.2 convolution_convert_fusion
  410.0 52.5 %reduce-scatter.6.cloned.1.call-done = bf16[128,1536]{1,0:T(8,128)(2,1)} async-done(((bf16[1024,1536]{1,0:T(8,128)(2,1)}), bf16[128,1536]{1,0:T(8,128)(2,1)}) %reduce-scatter.6.cloned.1.call-update) | async-done | bytes 393232 | tf_op jit(solution)/shard_map/reduce_scatter | solution.py:190
  464.6 40.5 %reduce-scatter.10.cloned.1.call-done = bf16[384,1030]{1,0:T(8,128)(2,1)} async-done(((bf16[1536,1030]{1,0:T(8,128)(2,1)}), bf16[384,1030]{1,0:T(8,128)(2,1)}) %reduce-scatter.10.cloned.1.call-update) | async-done | bytes 791056
  507.3 26.0 %reduce-scatter.8.cloned.1.call-done = bf16[96,1536]{1,0:T(8,128)(2,1)} async-done(((bf16[384,1536]{1,0:T(8,128)(2,1)}), bf16[96,1536]{1,0:T(8,128)(2,1)}) %reduce-scatter.8.cloned.1.call-update) | async-done | bytes 294928 | tf_op jit(solution)/shard_map/reduce_scatter | solution.py:205
  540.1 20.4 %all-to-all-done = bf16[8,128,384]{1,2,0:T(8,128)(2,1)S(1)} async-done(((bf16[8,128,384]{1,2,0:T(8,128)(2,1)}), bf16[8,128,384]{1,2,0:T(8,128)(2,1)S(1)}, u32[]{:S(2)}, u32[]{:S(2)}) %all-to-all-start) | async-done | bytes 786464 | tf_op jit(solution)/shard_map/all_to_all | solution.py:178
  567.8 95.1 %all-reduce.37.cloned.1.call-done = f32[21392]{0:T(1024)} async-done(((f32[21392]{0:T(1024)}), f32[21392]{0:T(1024)}) %all-reduce.37.cloned.1.call-update) | async-done | bytes 85584 | tf_op jit(solution)/shard_map/psum | solution.py:236
  671.3 96.4 %all-gather.21.cloned.1.call-done = bf16[3072,1030]{0,1:T(8,128)(2,1)} async-done(((bf16[384,1030]{0,1:T(8,128)(2,1)}), bf16[3072,1030]{0,1:T(8,128)(2,1)}) %all-gather.21.cloned.1.call-update) | async-done | bytes 6328336 | tf_op jit(solution)/shard_map/all_gather | solution.py:195
  767.7 9.0 %convert_element_type.81 = f32[3072,1030]{0,1:T(8,128)} convert(bf16[3072,1030]{0,1:T(8,128)(2,1)} %all-gather.21.cloned.1.call-done) | non-fusion elementwise | flops 3164160 | bytes 18984960 | tf_op jit(solution)/shard_map/convert_element_type | solution.py:195
  776.7 12.2 %copy.259 = f32[129,8,8,384]{3,2,1,0:T(8,128)} copy(f32[129,8,8,384]{3,1,2,0:T(8,128)} %bitcast.562) | data formatting | bytes 25362432
  799.7 8.1 slice_bitcast_fusion.2
  831.9 8.4 pad_maximum_fusion
  840.3 9.8 %all-gather.15.cloned.1.call-done = bf16[3072,1536]{1,0:T(8,128)(2,1)} async-done(((bf16[96,1536]{1,0:T(8,128)(2,1)}), bf16[3072,1536]{1,0:T(8,128)(2,1)}) %all-gather.15.cloned.1.call-update) | async-done | bytes 9437200 | tf_op jit(solution)/shard_map/all_gather | solution.py:206
  (578 shorter events, 202.7 us)
Async XLA Ops:
  7.2 65.8 %all-gather.17.cloned.1.call-start = ((), (), s32[]{:S(2)}) async-start(), calls=%async_computation.10 | async-start | bytes 3538944 | tf_op jit(solution)/shard_map/all_gather | solution.py:141
  7.9 96.7 %all-gather.11.cloned.1.call-start = ((), (), s32[]{:S(2)}) async-start(), calls=%async_computation.4 | async-start | bytes 4423680 | tf_op jit(solution)/shard_map/all_gather | solution.py:122
  10.5 156.5 %all-gather.19.cloned.1.call-start = ((), (), s32[]{:S(2)}) async-start(), calls=%async_computation.11 | async-start | bytes 3538944 | tf_op jit(solution)/shard_map/all_gather | solution.py:142
  11.2 220.1 %all-gather.13.cloned.1.call-start = ((), (), s32[]{:S(2)}) async-start(), calls=%async_computation.5 | async-start | bytes 11796480 | tf_op jit(solution)/shard_map/all_gather | solution.py:143
  11.8 450.7 %reduce-scatter.6.cloned.1.call-start = ((), (), s32[]{:S(2)}) async-start(), calls=%async_computation.6 | async-start | bytes 3538944 | tf_op jit(solution)/shard_map/reduce_scatter | solution.py:190
  27.6 77.0 %copy-start.64 = (f32[1536]{0:T(1024)}, f32[1536]{0:T(1024)S(1)}, u32[]{:S(2)}) copy-start(f32[1536]{0:T(1024)S(1)} %mul.709) | copy-start | bytes 18436
  29.2 86.2 %copy-start.143 = (f32[6]{0:T(128)}, f32[6]{0:T(128)S(1)}, u32[]{:S(2)}) copy-start(f32[6]{0:T(128)S(1)} %dynamic_slice.59) | copy-start | bytes 76
  29.3 46.5 %copy-start.139 = (f32[48]{0:T(128)}, f32[48]{0:T(128)S(1)}, u32[]{:S(2)}) copy-start(f32[48]{0:T(128)S(1)} %reshape.513) | copy-start | bytes 580
  30.0 80.8 %copy-start.83 = (f32[640]{0:T(1024)}, f32[640]{0:T(1024)S(1)}, u32[]{:S(2)}) copy-start(f32[640]{0:T(1024)S(1)} %get-tuple-element.58) | copy-start | bytes 7684
  30.0 80.8 %copy-start.85 = (f32[640]{0:T(1024)}, f32[640]{0:T(1024)S(1)}, u32[]{:S(2)}) copy-start(f32[640]{0:T(1024)S(1)} %get-tuple-element.59) | copy-start | bytes 7684
  30.1 85.5 %copy-start.127 = (f32[6]{0:T(128)}, f32[6]{0:T(128)S(1)}, u32[]{:S(2)}) copy-start(f32[6]{0:T(128)S(1)} %fusion.310) | copy-start | bytes 76
  73.1 31.6 %copy-start.22 = (bf16[1,1024,1536]{2,1,0:T(8,128)(2,1)S(1)}, bf16[1,1024,1536]{2,1,0:T(8,128)(2,1)}, u32[]{:S(2)}) copy-start(bf16[1,1024,1536]{2,1,0:T(8,128)(2,1)} %all-gather.17.cloned.1.call-done) | copy-start | bytes 9437188
  75.8 34.7 %copy-start.128 = (f32[1024]{0:T(1024)}, f32[1024]{0:T(1024)S(1)}, u32[]{:S(2)}) copy-start(f32[1024]{0:T(1024)S(1)} %add_rsqrt_fusion) | copy-start | bytes 12292
  237.3 28.9 %copy-start.35 = (bf16[1024,384]{0,1:T(8,128)(2,1)}, bf16[1024,384]{0,1:T(8,128)(2,1)S(1)}, u32[]{:S(2)}) copy-start(bf16[1024,384]{0,1:T(8,128)(2,1)S(1)} %get-tuple-element.65) | copy-start | bytes 2359300
  294.6 35.5 %copy-start.94 = (f32[256,6]{0,1:T(8,128)S(1)}, f32[256,6]{0,1:T(8,128)}, u32[]{:S(2)}) copy-start(f32[256,6]{0,1:T(8,128)} %multiply_reduce_fusion.17) | copy-start | bytes 18436
  294.6 44.8 %copy-start.63 = (f32[1,6,2,128]{3,2,1,0:T(2,128)S(1)}, f32[1,6,2,128]{3,2,1,0:T(2,128)}, u32[]{:S(2)}) copy-start(f32[1,6,2,128]{3,2,1,0:T(2,128)} %copy-done.62) | copy-start | bytes 18436
  294.6 44.8 %copy-start.89 = (f32[256,6]{0,1:T(8,128)S(1)}, f32[256,6]{0,1:T(8,128)}, u32[]{:S(2)}) copy-start(f32[256,6]{0,1:T(8,128)} %multiply_reduce_fusion.19) | copy-start | bytes 18436
  391.8 113.3 %reduce-scatter.10.cloned.1.call-start = ((), (), s32[]{:S(2)}) async-start(), calls=%async_computation.13 | async-start | bytes 4423680
  402.4 130.9 %reduce-scatter.8.cloned.1.call-start = ((), (), s32[]{:S(2)}) async-start(), calls=%async_computation.8 | async-start | bytes 1474560 | tf_op jit(solution)/shard_map/reduce_scatter | solution.py:205
  407.9 255.0 %all-reduce.37.cloned.1.call-start = ((), (), s32[]{:S(2)}) async-start(), calls=%async_computation.7 | async-start | bytes 172032 | tf_op jit(solution)/shard_map/psum | solution.py:236
  463.8 69.5 %copy-start.21 = (bf16[48,8,8,128]{3,2,1,0:T(8,128)(2,1)S(1)}, bf16[48,8,8,128]{3,2,1,0:T(8,128)(2,1)}, u32[]{:S(2)}) copy-start(bf16[48,8,8,128]{3,2,1,0:T(8,128)(2,1)} %get-tuple-element.85) | copy-start | bytes 2359300
  464.5 303.2 %all-gather.21.cloned.1.call-start = ((), (), s32[]{:S(2)}) async-start(), calls=%async_computation.12 | async-start | bytes 7133184 | tf_op jit(solution)/shard_map/all_gather | solution.py:195
  507.3 342.8 %all-gather.15.cloned.1.call-start = ((), (), s32[]{:S(2)}) async-start(), calls=%async_computation.9 | async-start | bytes 9732096 | tf_op jit(solution)/shard_map/all_gather | solution.py:206
  534.4 26.2 %all-to-all-start = ((bf16[8,128,384]{1,2,0:T(8,128)(2,1)}), bf16[8,128,384]{1,2,0:T(8,128)(2,1)S(1)}, u32[]{:S(2)}, u32[]{:S(2)}) async-start(bf16[8,128,384]{1,2,0:T(8,128)(2,1)} %bitcast.553), calls=%async_computation | async-start | bytes 1572864 | tf_op jit(solution)/shard_map/all_to_all | solution.py:178
  (139 other events, 453.5 us)
Sparse Core Ops, SparseCore 0:
  10.2 62.8 all-gather.16
  75.2 29.3 all-gather.10
  106.8 60.0 all-gather.18
  168.3 62.8 all-gather.12
  391.9 70.5 reduce-scatter.5
  465.5 39.5 reduce-scatter.9
  507.6 25.6 reduce-scatter.7
  539.4 123.3 all-reduce.36
  665.5 102.1 all-gather.20
  770.5 79.6 all-gather.14
where the time goes:
time: 870 us; the launch traced here: 862 us
  waiting for transfers between devices  511 us (59%)
  other arithmetic  116 us (13%)
  local copies, waits for them, and re-layouts  100 us (11%)
  matrix products  75.5 us (9%)
  blocking collectives  35.9 us (4%)
  between operations  17.3 us (2%)
    all_gather x1, waiting for transfers between devices, shards(): in_all = lax.all_gather(in_red, 'seq', axis=0, tiled=False).astype(f32)  96.4 us
    psum x1, waiting for transfers between devices, shards(): packed = lax.psum(packed, ('seq', 'fsdp'))  95.1 us
    all_gather x1, waiting for transfers between devices, shards(): w_out = lax.all_gather(out_weight, 'fsdp', axis=0, tiled=True)  64.3 us
    reduce_scatter x1, waiting for transfers between devices, shards(): lax.psum_scatter(hid_part.astype(bf16), 'seq', scatter_dimension=0, tiled...  52.5 us
    another operation x17, other arithmetic  49.7 us
    unnamed x11, waiting for transfers between devices  42.5 us
    all_gather x1, waiting for transfers between devices, shards(): tok = lax.all_gather(tokens[0], 'seq', axis=0, tiled=True)  42.3 us
    unnamed x312, local copies, waits for them, and re-layouts  41.4 us
  transfers between devices with their start and end apart: 11, of which 11 were waited for; matrix products, arithmetic and copies ran while one was open for 17% of the time, Pallas kernels for 0%

commit v1 on v0

--- a/solution.py
+++ b/solution.py
@@ -140,7 +140,12 @@
     norm_f = take(width // fs).reshape(-1)
     tok = lax.all_gather(tokens[0], "seq", axis=0, tiled=True)
     cot = lax.all_gather(cotangent[0], "seq", axis=0, tiled=True)
-    w_out = lax.all_gather(out_weight, "fsdp", axis=0, tiled=True)
+    ring = [out_weight]
+    for hop in range(3):
+        ring.append(lax.ppermute(ring[-1], "fsdp", [(dev, (dev + 1) % 4) for dev in range(4)]))
+    w_out = jnp.roll(
+        jnp.concatenate(ring[::-1], axis=0), (lax.axis_index("fsdp") + 1) * ring[0].shape[0], axis=0
+    )
     w_out_g = sl(w_out, col, cols, 0)
     length = tok.shape[0]
     own = length // seqs

time: 870 us -> 802 us (0.922)
  waiting for transfers between devices: 511 us -> 414 us
  local copies, waits for them, and re-layouts: 100 us -> 118 us
  blocking collectives: 35.9 us -> 53 us
  other arithmetic: 116 us -> 103 us
    all_gather x1 -> x0, waiting for transfers between devices: 64.3 us -> none  [shards(): w_out = lax.all_gather(out_weight, 'fsdp', axis=0, tiled=True)]
    all_gather x1, waiting for transfers between devices: 42.3 us -> 0.01 us  [shards(): tok = lax.all_gather(tokens[0], 'seq', axis=0, tiled=True)]
    ppermute x0 -> x3, waiting for transfers between devices: none -> 28.6 us  [shards(): lax.ppermute(ring[-1], 'fsdp', [(dev, (dev + 1) % 4) for dev in range(4)])]
    all_gather x1, waiting for transfers between devices: 32.4 us -> 7.87 us  [shards(): cot = lax.all_gather(cotangent[0], 'seq', axis=0, tiled=True)]
    unnamed x312 -> x339, local copies, waits for them, and re-layouts: 41.4 us -> 62.4 us
    unnamed x1, blocking collectives: 13.6 us -> 32.6 us
    unnamed x11 -> x10, waiting for transfers between devices: 42.5 us -> 41.3 us
  transfers between devices with their start and end apart: 11 -> 13, of which waited for: 11 -> 10; matrix products, arithmetic and copies ran while one was open for 17% -> 21% of each run, Pallas kernels for 0% -> 0%
where the time goes in v1:
time: 802 us; the launch traced here: 795 us
  waiting for transfers between devices  414 us (52%)
  local copies, waits for them, and re-layouts  118 us (15%)
  other arithmetic  103 us (13%)
  matrix products  82.4 us (10%)
  blocking collectives  53 us (7%)
  between operations  17.3 us (2%)
    all_gather x1, waiting for transfers between devices, shards(): in_all = lax.all_gather(in_red, 'seq', axis=0, tiled=False).astype(f32)  96.4 us
    psum x1, waiting for transfers between devices, shards(): packed = lax.psum(packed, ('seq', 'fsdp'))  93.5 us
    unnamed x339, local copies, waits for them, and re-layouts  62.4 us
    reduce_scatter x1, waiting for transfers between devices, shards(): lax.psum_scatter(hid_part.astype(bf16), 'seq', scatter_dimension=0, tiled...  53.7 us
    another operation x17, other arithmetic  42.6 us
    unnamed x10, waiting for transfers between devices  41.3 us
    dot_general x6, matrix products, contract(): lax.dot_general(left, right, (((left_dim,), (right_dim,)), ((), ())), pre...  36.1 us
    all_gather x1, waiting for transfers between devices, shards(): w_g = lax.all_gather(w_part, 'fsdp', axis=0, tiled=True)  33.4 us
  transfers between devices with their start and end apart: 13, of which 10 were waited for; matrix products, arithmetic and copies ran while one was open for 21% of the time, Pallas kernels for 0%

profile of v1, /device:TPU:0, one launch (start us, length us, event | category | flops | bytes accessed | tf_op | source)
XLA Modules:
  0.0 794.8 jit_solution(13595292609054639683)
XLA Ops:
  11.2 28.6 %collective-permute-done = bf16[768,1536]{1,0:T(8,128)(2,1)} collective-permute-done((bf16[768,1536]{1,0:T(8,128)(2,1)S(1)}, bf16[768,1536]{1,0:T(8,128)(2,1)}, u32[]{:S(2)}, u32[]{:S(2)}) %collective-permute-start) | collective-permute-done | bytes 2359328 | tf_op jit(solution)/shard_map/ppermute | solution.py:145
  41.8 32.6 %all-reduce.34 = bf16[21392]{0:T(1024)(128)(2,1)S(1)} all-reduce(bf16[21392]{0:T(1024)(128)(2,1)S(1)} %dynamic-update-slice), channel_id=2, replica_groups=mesh['seq'=8,'fsdp'=4] {'fsdp'}, use_global_device_ids=true, to_apply=%add.34 | all-reduce | flops 21392 | bytes 85568
  80.8 33.4 %all-gather.10.cloned.1.call-done = bf16[1536,1030]{1,0:T(8,128)(2,1)} async-done(((bf16[384,1030]{1,0:T(8,128)(2,1)}), bf16[1536,1030]{1,0:T(8,128)(2,1)}) %all-gather.10.cloned.1.call-update) | async-done | bytes 3164176 | tf_op jit(solution)/shard_map/all_gather | solution.py:122
  168.8 7.9 all-gather.16.cloned.1.call-done
  176.7 6.0 fusion.29
  183.4 20.4 %psum.14 = f32[2,1024]{1,0:T(2,128)} all-reduce(f32[2,1024]{1,0:T(2,128)} %pad_maximum_fusion.6), channel_id=1, replica_groups=mesh['seq'=8,'fsdp'=4] {'seq'}, use_global_device_ids=true, to_apply=%region_11.12 | all-reduce | flops 2048 | bytes 16384 | tf_op jit(solution)/shard_map/psum | solution.py:178
  231.1 8.8 %reduce-window.66 = f32[6,2,128]{2,1,0:T(2,128)} reduce-window(f32[6,2,128]{2,1,0:T(2,128)} %reshape.527, f32[]{:T(128)} %constant.91.clone.1), window={size=1x1x128 pad=0_0x0_0x0_127}, to_apply=%region_21.22 | reduce-window | flops 195072 | bytes 12292 | tf_op jit(solution)/shard_map/reduce-window.8
  258.8 7.6 reduce-window.74
  270.7 7.6 reduce-window.76
  278.6 7.7 reduce-window.70
  324.8 6.2 convolution_convert_fusion
  342.2 53.7 %reduce-scatter.6.cloned.1.call-done = bf16[128,1536]{1,0:T(8,128)(2,1)} async-done(((bf16[1024,1536]{1,0:T(8,128)(2,1)}), bf16[128,1536]{1,0:T(8,128)(2,1)}) %reduce-scatter.6.cloned.1.call-update) | async-done | bytes 393232 | tf_op jit(solution)/shard_map/reduce_scatter | solution.py:195
  397.9 40.5 %reduce-scatter.10.cloned.1.call-done = bf16[384,1030]{1,0:T(8,128)(2,1)} async-done(((bf16[1536,1030]{1,0:T(8,128)(2,1)}), bf16[384,1030]{1,0:T(8,128)(2,1)}) %reduce-scatter.10.cloned.1.call-update) | async-done | bytes 791056
  440.6 25.8 %reduce-scatter.8.cloned.1.call-done = bf16[96,1536]{1,0:T(8,128)(2,1)} async-done(((bf16[384,1536]{1,0:T(8,128)(2,1)}), bf16[96,1536]{1,0:T(8,128)(2,1)}) %reduce-scatter.8.cloned.1.call-update) | async-done | bytes 294928 | tf_op jit(solution)/shard_map/reduce_scatter | solution.py:210
  473.2 20.4 %all-to-all-done = bf16[8,128,384]{1,2,0:T(8,128)(2,1)S(1)} async-done(((bf16[8,128,384]{1,2,0:T(8,128)(2,1)}), bf16[8,128,384]{1,2,0:T(8,128)(2,1)S(1)}, u32[]{:S(2)}, u32[]{:S(2)}) %all-to-all-start) | async-done | bytes 786464 | tf_op jit(solution)/shard_map/all_to_all | solution.py:183
  493.7 7.5 fusion.23
  502.4 93.5 %all-reduce.37.cloned.1.call-done = f32[21392]{0:T(1024)} async-done(((f32[21392]{0:T(1024)}), f32[21392]{0:T(1024)}) %all-reduce.37.cloned.1.call-update) | async-done | bytes 85584 | tf_op jit(solution)/shard_map/psum | solution.py:241
  604.3 96.4 %all-gather.18.cloned.1.call-done = bf16[3072,1030]{0,1:T(8,128)(2,1)} async-done(((bf16[384,1030]{0,1:T(8,128)(2,1)}), bf16[3072,1030]{0,1:T(8,128)(2,1)}) %all-gather.18.cloned.1.call-update) | async-done | bytes 6328336 | tf_op jit(solution)/shard_map/all_gather | solution.py:200
  700.7 9.0 %convert_element_type.81 = f32[3072,1030]{0,1:T(8,128)} convert(bf16[3072,1030]{0,1:T(8,128)(2,1)} %all-gather.18.cloned.1.call-done) | non-fusion elementwise | flops 3164160 | bytes 18984960 | tf_op jit(solution)/shard_map/convert_element_type | solution.py:200
  709.7 12.3 %copy.259 = f32[129,8,8,384]{3,2,1,0:T(8,128)} copy(f32[129,8,8,384]{3,1,2,0:T(8,128)} %bitcast.561) | data formatting | bytes 25362432
  734.6 6.1 copy.196
  746.1 6.3 copy.197
  761.5 8.5 %pad_maximum_fusion = f32[384,6400]{1,0:T(8,128)} fusion(f32[384,256]{1,0:T(8,128)S(1)} %copy.198, f32[384,3072]{1,0:T(8,128)} %bitcast.566, f32[384,3072]{1,0:T(8,128)} %bitcast.565), kind=kLoop, calls=%fused_computation.1 | loop fusion | flops 4915200 | bytes 19660800 | tf_op jit(solution)/shard_map/concatenate | solution.py:201
  770.0 13.2 %all-gather.12.cloned.1.call-done = bf16[3072,1536]{1,0:T(8,128)(2,1)} async-done(((bf16[96,1536]{1,0:T(8,128)(2,1)}), bf16[3072,1536]{1,0:T(8,128)(2,1)}) %all-gather.12.cloned.1.call-update) | async-done | bytes 9437200 | tf_op jit(solution)/shard_map/all_gather | solution.py:211
  (610 shorter events, 217.5 us)
Async XLA Ops:
  7.2 70.8 %all-gather.14.cloned.1.call-start = ((), (), s32[]{:S(2)}) async-start(), calls=%async_computation.9 | async-start | bytes 3538944 | tf_op jit(solution)/shard_map/all_gather | solution.py:141
  7.9 106.3 %all-gather.10.cloned.1.call-start = ((), (), s32[]{:S(2)}) async-start(), calls=%async_computation.4 | async-start | bytes 4423680 | tf_op jit(solution)/shard_map/all_gather | solution.py:122
  8.2 33.0 %copy-start.148 = (bf16[832]{0:T(1024)(128)(2,1)S(1)}, bf16[832]{0:T(1024)(128)(2,1)}, u32[]{:S(2)}) copy-start(bf16[832]{0:T(1024)(128)(2,1)} %param.16) | copy-start | bytes 4996
  8.3 33.0 %copy-start.149 = (bf16[768]{0:T(1024)(128)(2,1)S(1)}, bf16[768]{0:T(1024)(128)(2,1)}, u32[]{:S(2)}) copy-start(bf16[768]{0:T(1024)(128)(2,1)} %param.20) | copy-start | bytes 4612
  10.6 166.1 %all-gather.16.cloned.1.call-start = ((), (), s32[]{:S(2)}) async-start(), calls=%async_computation.10 | async-start | bytes 3538944 | tf_op jit(solution)/shard_map/all_gather | solution.py:142
  10.7 29.1 %collective-permute-start = (bf16[768,1536]{1,0:T(8,128)(2,1)S(1)}, bf16[768,1536]{1,0:T(8,128)(2,1)}, u32[]{:S(2)}, u32[]{:S(2)}) collective-permute-start(bf16[768,1536]{1,0:T(8,128)(2,1)S(1)} %copy-done.17), channel_id=1, source_target_pairs={{0,1},{1,2},{2,3},{3,0},{4,5},{5,6},{6,7},{7,4},{8,9},{9,10},{10,1... | collective-permute-start | bytes 7077896 | tf_op jit(solution)/shard_map/ppermute | solution.py:145
  39.8 38.0 %collective-permute-start.1 = (bf16[768,1536]{1,0:T(8,128)(2,1)}, bf16[768,1536]{1,0:T(8,128)(2,1)}, u32[]{:S(2)}, u32[]{:S(2)}) collective-permute-start(bf16[768,1536]{1,0:T(8,128)(2,1)} %collective-permute-done), channel_id=1, source_target_pairs={{0,1},{1,2},{2,3},{3,0},{4,5},{5,6},{6,7},{7,4},{8,9},{9,10},{10,1... | collective-permute-start | bytes 7077896 | tf_op jit(solution)/shard_map/ppermute | solution.py:145
  39.8 356.0 %reduce-scatter.6.cloned.1.call-start = ((), (), s32[]{:S(2)}) async-start(), calls=%async_computation.5 | async-start | bytes 3538944 | tf_op jit(solution)/shard_map/reduce_scatter | solution.py:195
  74.7 45.5 %copy-start.67 = (f32[1536]{0:T(1024)}, f32[1536]{0:T(1024)S(1)}, u32[]{:S(2)}) copy-start(f32[1536]{0:T(1024)S(1)} %mul.712) | copy-start | bytes 18436
  74.9 52.8 %copy-start.150 = (f32[6]{0:T(128)}, f32[6]{0:T(128)S(1)}, u32[]{:S(2)}) copy-start(f32[6]{0:T(128)S(1)} %dynamic_slice.66) | copy-start | bytes 76
  75.0 45.2 %copy-start.146 = (f32[48]{0:T(128)}, f32[48]{0:T(128)S(1)}, u32[]{:S(2)}) copy-start(f32[48]{0:T(128)S(1)} %reshape.513) | copy-start | bytes 580
  77.1 43.3 %copy-start.86 = (f32[640]{0:T(1024)}, f32[640]{0:T(1024)S(1)}, u32[]{:S(2)}) copy-start(f32[640]{0:T(1024)S(1)} %get-tuple-element.58) | copy-start | bytes 7684
  77.1 43.3 %copy-start.88 = (f32[640]{0:T(1024)}, f32[640]{0:T(1024)S(1)}, u32[]{:S(2)}) copy-start(f32[640]{0:T(1024)S(1)} %get-tuple-element.59) | copy-start | bytes 7684
  77.2 50.7 %copy-start.138 = (f32[6]{0:T(128)}, f32[6]{0:T(128)S(1)}, u32[]{:S(2)}) copy-start(f32[6]{0:T(128)S(1)} %fusion.320) | copy-start | bytes 76
  77.8 68.0 %collective-permute-start.2 = (bf16[768,1536]{1,0:T(8,128)(2,1)}, bf16[768,1536]{1,0:T(8,128)(2,1)}, u32[]{:S(2)}, u32[]{:S(2)}) collective-permute-start(bf16[768,1536]{1,0:T(8,128)(2,1)} %collective-permute-done.1), channel_id=1, source_target_pairs={{0,1},{1,2},{2,3},{3,0},{4,5},{5,6},{6,7},{7,4},{8,9},{9,10},{10,1... | collective-permute-start | bytes 7077896 | tf_op jit(solution)/shard_map/ppermute | solution.py:145
  78.0 36.3 %copy-start.26 = (bf16[1,1024,1536]{2,1,0:T(8,128)(2,1)S(1)}, bf16[1,1024,1536]{2,1,0:T(8,128)(2,1)}, u32[]{:S(2)}) copy-start(bf16[1,1024,1536]{2,1,0:T(8,128)(2,1)} %all-gather.14.cloned.1.call-done) | copy-start | bytes 9437188
  80.8 39.4 %copy-start.140 = (f32[1024]{0:T(1024)}, f32[1024]{0:T(1024)S(1)}, u32[]{:S(2)}) copy-start(f32[1024]{0:T(1024)S(1)} %add_rsqrt_fusion) | copy-start | bytes 12292
  324.1 114.2 %reduce-scatter.10.cloned.1.call-start = ((), (), s32[]{:S(2)}) async-start(), calls=%async_computation.12 | async-start | bytes 4423680
  334.8 131.6 %reduce-scatter.8.cloned.1.call-start = ((), (), s32[]{:S(2)}) async-start(), calls=%async_computation.7 | async-start | bytes 1474560 | tf_op jit(solution)/shard_map/reduce_scatter | solution.py:210
  340.3 255.6 %all-reduce.37.cloned.1.call-start = ((), (), s32[]{:S(2)}) async-start(), calls=%async_computation.6 | async-start | bytes 172032 | tf_op jit(solution)/shard_map/psum | solution.py:241
  340.6 125.8 %copy-start.25 = (bf16[48,8,8,128]{3,2,1,0:T(8,128)(2,1)S(1)}, bf16[48,8,8,128]{3,2,1,0:T(8,128)(2,1)}, u32[]{:S(2)}) copy-start(bf16[48,8,8,128]{3,2,1,0:T(8,128)(2,1)} %get-tuple-element.85) | copy-start | bytes 2359300
  397.8 302.8 %all-gather.18.cloned.1.call-start = ((), (), s32[]{:S(2)}) async-start(), calls=%async_computation.11 | async-start | bytes 7133184 | tf_op jit(solution)/shard_map/all_gather | solution.py:200
  440.5 342.7 %all-gather.12.cloned.1.call-start = ((), (), s32[]{:S(2)}) async-start(), calls=%async_computation.8 | async-start | bytes 9732096 | tf_op jit(solution)/shard_map/all_gather | solution.py:211
  467.4 26.2 %all-to-all-start = ((bf16[8,128,384]{1,2,0:T(8,128)(2,1)}), bf16[8,128,384]{1,2,0:T(8,128)(2,1)S(1)}, u32[]{:S(2)}, u32[]{:S(2)}) async-start(bf16[8,128,384]{1,2,0:T(8,128)(2,1)} %bitcast.552), calls=%async_computation | async-start | bytes 1572864 | tf_op jit(solution)/shard_map/all_to_all | solution.py:183
  (151 other events, 823.0 us)
Sparse Core Ops, SparseCore 0:
  10.2 62.7 all-gather.13
  75.1 39.0 all-gather.9
  116.4 60.1 all-gather.15
  324.3 71.5 reduce-scatter.5
  398.8 39.4 reduce-scatter.9
  440.8 25.5 reduce-scatter.7
  472.5 123.2 all-reduce.36
  598.5 102.1 all-gather.17
  703.6 79.6 all-gather.11
